TPU v7x, 32 devices: a whole 2x2x4 slice. The times are simulated.
32 devices in a mesh: freq: 2 (over x), base: 4 (over y, core), pix: 4 (over z).
Axes of the slice: x: 2, y: 2, z: 4, core: 2. Of those that a mesh axis runs over, the one named last changes fastest.
Arguments:
- sensing_operator_parts: bfloat16 [2, 4096, 2048], P('freq', 'base', 'pix'), may hold values from -1 to 1
- sampled_correlations: float32 [64, 4096], P('freq', 'base'), may hold values from -40 to 40
- first_sky_estimate: float32 [64, 4, 4, 128], P('freq', 'pix', 'base'), may hold values from -2.5 to 2.5
- patch_order_record: int32 [6, 16], P(None, 'pix'), may hold values from 0 to 15, as said below
Outputs:
- image: float32 [64, 4, 4, 128], P('freq', 'pix', 'base')
Inputs may be any that keep to these rules, and one draw needn't show every extreme that they name: `patch_order_record`: each row holds every tile number once; the tiles of rank under 4 are the same in every row.
All inputs are finite; a program needn't handle non-finite values.
Results may differ from a plain program's by a relative error of at most 0.0014.
Values may be sent and summed in bfloat16 or wider, within the bound.
No kernel may reach another device: no remote copies, remote signals or barrier semaphores. Data moves between devices by JAX's collectives and lax.ppermute only.
A program may use at most 64 MiB of HBM per device.

v0:
```python
import jax
import jax.numpy as jnp
from jax import lax
from jax.sharding import PartitionSpec as P

CH = 64
TILE = 128
ITERS = 6
descent_stride = 0.6
lam_shrink = 0.3
eps_norm = 1e-06


def project_rows(rounded_amount, columns):
    return lax.dot_general(
        rounded_amount, columns, (((1,), (1,)), ((), ())), preferred_element_type=jnp.float32
    )


def residual_of(sampled_correlations, partial_value):
    shares = lax.psum_scatter(partial_value, "pix", scatter_dimension=1, tiled=True)
    width = shares.shape[1]
    own_rows = lax.dynamic_slice_in_dim(
        sampled_correlations, lax.axis_index("pix") * width, width, 1
    )
    return lax.all_gather((own_rows - shares).astype(jnp.bfloat16), "pix", axis=1, tiled=True)


def on_device(sensing_operator_parts, sampled_correlations, first_sky_estimate, patch_order_record):
    sensing_operator = sensing_operator_parts[0]
    chans, m_dev = sampled_correlations.shape
    share_width = first_sky_estimate.shape[3]
    tiles_share = share_width // TILE
    keep_count = tiles_share * lax.axis_size("base") * lax.axis_size("pix") // 4
    base_index = lax.axis_index("base")
    own_share = first_sky_estimate[:, 0, 0, :]
    current = own_share
    for step in range(ITERS):
        rounded_amount = current.astype(jnp.bfloat16)
        partial_value = project_rows(
            lax.all_gather(rounded_amount, "base", axis=1, tiled=True), sensing_operator
        )
        resid = residual_of(sampled_correlations, partial_value)
        gradient_portion = jnp.dot(resid, sensing_operator, preferred_element_type=jnp.float32)
        grad_share = lax.psum_scatter(gradient_portion, "base", scatter_dimension=1, tiled=True)
        moved = current + descent_stride * grad_share
        tiles = moved.reshape(chans, tiles_share, TILE)
        local_sum = jnp.sum(tiles * tiles, axis=(0, 2))
        total = lax.psum(local_sum, "freq")
        ranks = lax.dynamic_slice_in_dim(
            patch_order_record[step], base_index * tiles_share, tiles_share, 0
        )
        rms_tile = jnp.sqrt(total / (CH * TILE) + eps_norm)
        keeping = (ranks < keep_count).astype(jnp.float32)
        factor = keeping * rms_tile / (rms_tile + lam_shrink)
        current = (tiles * factor[None, :, None]).reshape(chans, share_width)
    return current.reshape(chans, 1, 1, share_width)


def solution(mesh):
    in_specs = (
        P("freq", "base", "pix"),
        P("freq", "base"),
        P("freq", "pix", "base", None),
        P(None, "pix"),
    )
    out_specs = P("freq", "pix", "base", None)
    return jax.shard_map(
        on_device, mesh=mesh, in_specs=in_specs, out_specs=out_specs, check_vma=False
    )
```

profile of v0, /device:TPU:0, one launch (start us, length us, event | category | flops | bytes accessed | tf_op | source)
XLA Modules:
  0.0 418.8 jit_solution(5193370528719612826)
XLA Ops:
  7.3 6.1 %all_gather.36 = bf16[32,512]{1,0:T(8,128)(2,1)S(1)} all-gather(bf16[32,128]{1,0:T(8,128)(2,1)S(1)} %convert_element_type.42), channel_id=1, replica_groups=mesh['freq'=2,'base'=4,'pix'=4] {'base'}, dimensions={1}, use_global_device_ids=true | all-gather | bytes 40960 | tf_op jit(solution)/shard_map/all_gather | solution.py:41
  14.6 21.3 %reduce-scatter.13.cloned.1.call-done = f32[32,256]{1,0:T(8,128)} async-done(((f32[32,1024]{1,0:T(8,128)}), f32[32,256]{1,0:T(8,128)}) %reduce-scatter.13.cloned.1.call-update) | async-done | bytes 32784 | tf_op jit(solution)/shard_map/reduce_scatter | solution.py:21
  36.7 13.1 %all_gather.37 = bf16[32,1024]{1,0:T(8,128)(2,1)S(1)} all-gather(bf16[32,256]{1,0:T(8,128)(2,1)S(1)} %subtract_convert_fusion.5), channel_id=1, replica_groups=mesh['freq'=2,'base'=4,'pix'=4] {'pix'}, dimensions={1}, use_global_device_ids=true | all-gather | bytes 81920 | tf_op jit(solution)/shard_map/all_gather | solution.py:26
  52.0 16.6 %reduce-scatter.15.cloned.1.call-done = f32[32,128]{1,0:T(8,128)} async-done(((f32[32,512]{1,0:T(8,128)}), f32[32,128]{1,0:T(8,128)}) %reduce-scatter.15.cloned.1.call-update) | async-done | bytes 16400 | tf_op jit(solution)/shard_map/reduce_scatter | solution.py:45
  70.0 5.5 %psum.42 = f32[1]{0:T(128)} all-reduce(f32[1]{0:T(128)} %bitcast.3), channel_id=1, replica_groups=mesh['freq'=2,'base'=4,'pix'=4] {'freq'}, use_global_device_ids=true, to_apply=%region_3.0 | all-reduce | flops 1 | bytes 8 | tf_op jit(solution)/shard_map/psum | solution.py:49
  83.2 19.6 %reduce-scatter.17.cloned.1.call-done = f32[32,256]{1,0:T(8,128)} async-done(((f32[32,1024]{1,0:T(8,128)}), f32[32,256]{1,0:T(8,128)}) %reduce-scatter.17.cloned.1.call-update) | async-done | bytes 32784 | tf_op jit(solution)/shard_map/reduce_scatter | solution.py:21
  103.5 13.1 %all_gather.39 = bf16[32,1024]{1,0:T(8,128)(2,1)S(1)} all-gather(bf16[32,256]{1,0:T(8,128)(2,1)S(1)} %subtract_convert_fusion.4), channel_id=1, replica_groups=mesh['freq'=2,'base'=4,'pix'=4] {'pix'}, dimensions={1}, use_global_device_ids=true | all-gather | bytes 81920 | tf_op jit(solution)/shard_map/all_gather | solution.py:26
  118.2 17.3 %reduce-scatter.19.cloned.1.call-done = f32[32,128]{1,0:T(8,128)} async-done(((f32[32,512]{1,0:T(8,128)}), f32[32,128]{1,0:T(8,128)}) %reduce-scatter.19.cloned.1.call-update) | async-done | bytes 16400 | tf_op jit(solution)/shard_map/reduce_scatter | solution.py:45
  136.9 5.5 %psum.43 = f32[1]{0:T(128)} all-reduce(f32[1]{0:T(128)} %bitcast.6), channel_id=1, replica_groups=mesh['freq'=2,'base'=4,'pix'=4] {'freq'}, use_global_device_ids=true, to_apply=%region_7.0 | all-reduce | flops 1 | bytes 8 | tf_op jit(solution)/shard_map/psum | solution.py:49
  150.1 19.6 %reduce-scatter.21.cloned.1.call-done = f32[32,256]{1,0:T(8,128)} async-done(((f32[32,1024]{1,0:T(8,128)}), f32[32,256]{1,0:T(8,128)}) %reduce-scatter.21.cloned.1.call-update) | async-done | bytes 32784 | tf_op jit(solution)/shard_map/reduce_scatter | solution.py:21
  170.5 13.1 %all_gather.41 = bf16[32,1024]{1,0:T(8,128)(2,1)S(1)} all-gather(bf16[32,256]{1,0:T(8,128)(2,1)S(1)} %subtract_convert_fusion.3), channel_id=1, replica_groups=mesh['freq'=2,'base'=4,'pix'=4] {'pix'}, dimensions={1}, use_global_device_ids=true | all-gather | bytes 81920 | tf_op jit(solution)/shard_map/all_gather | solution.py:26
  185.1 17.3 %reduce-scatter.23.cloned.1.call-done = f32[32,128]{1,0:T(8,128)} async-done(((f32[32,512]{1,0:T(8,128)}), f32[32,128]{1,0:T(8,128)}) %reduce-scatter.23.cloned.1.call-update) | async-done | bytes 16400 | tf_op jit(solution)/shard_map/reduce_scatter | solution.py:45
  203.8 5.5 %psum.44 = f32[1]{0:T(128)} all-reduce(f32[1]{0:T(128)} %bitcast.9), channel_id=1, replica_groups=mesh['freq'=2,'base'=4,'pix'=4] {'freq'}, use_global_device_ids=true, to_apply=%region_11.0 | all-reduce | flops 1 | bytes 8 | tf_op jit(solution)/shard_map/psum | solution.py:49
  217.0 19.6 %reduce-scatter.25.cloned.1.call-done = f32[32,256]{1,0:T(8,128)} async-done(((f32[32,1024]{1,0:T(8,128)}), f32[32,256]{1,0:T(8,128)}) %reduce-scatter.25.cloned.1.call-update) | async-done | bytes 32784 | tf_op jit(solution)/shard_map/reduce_scatter | solution.py:21
  237.3 13.1 %all_gather.43 = bf16[32,1024]{1,0:T(8,128)(2,1)S(1)} all-gather(bf16[32,256]{1,0:T(8,128)(2,1)S(1)} %subtract_convert_fusion.2), channel_id=1, replica_groups=mesh['freq'=2,'base'=4,'pix'=4] {'pix'}, dimensions={1}, use_global_device_ids=true | all-gather | bytes 81920 | tf_op jit(solution)/shard_map/all_gather | solution.py:26
  252.0 17.3 %reduce-scatter.27.cloned.1.call-done = f32[32,128]{1,0:T(8,128)} async-done(((f32[32,512]{1,0:T(8,128)}), f32[32,128]{1,0:T(8,128)}) %reduce-scatter.27.cloned.1.call-update) | async-done | bytes 16400 | tf_op jit(solution)/shard_map/reduce_scatter | solution.py:45
  270.7 5.5 %psum.45 = f32[1]{0:T(128)} all-reduce(f32[1]{0:T(128)} %bitcast.12), channel_id=1, replica_groups=mesh['freq'=2,'base'=4,'pix'=4] {'freq'}, use_global_device_ids=true, to_apply=%region_15.0 | all-reduce | flops 1 | bytes 8 | tf_op jit(solution)/shard_map/psum | solution.py:49
  283.9 19.6 %reduce-scatter.29.cloned.1.call-done = f32[32,256]{1,0:T(8,128)} async-done(((f32[32,1024]{1,0:T(8,128)}), f32[32,256]{1,0:T(8,128)}) %reduce-scatter.29.cloned.1.call-update) | async-done | bytes 32784 | tf_op jit(solution)/shard_map/reduce_scatter | solution.py:21
  304.2 13.1 %all_gather.45 = bf16[32,1024]{1,0:T(8,128)(2,1)S(1)} all-gather(bf16[32,256]{1,0:T(8,128)(2,1)S(1)} %subtract_convert_fusion.1), channel_id=1, replica_groups=mesh['freq'=2,'base'=4,'pix'=4] {'pix'}, dimensions={1}, use_global_device_ids=true | all-gather | bytes 81920 | tf_op jit(solution)/shard_map/all_gather | solution.py:26
  318.9 17.3 %reduce-scatter.31.cloned.1.call-done = f32[32,128]{1,0:T(8,128)} async-done(((f32[32,512]{1,0:T(8,128)}), f32[32,128]{1,0:T(8,128)}) %reduce-scatter.31.cloned.1.call-update) | async-done | bytes 16400 | tf_op jit(solution)/shard_map/reduce_scatter | solution.py:45
  337.6 5.5 %psum.46 = f32[1]{0:T(128)} all-reduce(f32[1]{0:T(128)} %bitcast.15), channel_id=1, replica_groups=mesh['freq'=2,'base'=4,'pix'=4] {'freq'}, use_global_device_ids=true, to_apply=%region_19.0 | all-reduce | flops 1 | bytes 8 | tf_op jit(solution)/shard_map/psum | solution.py:49
  350.8 19.6 %reduce-scatter.33.cloned.1.call-done = f32[32,256]{1,0:T(8,128)} async-done(((f32[32,1024]{1,0:T(8,128)}), f32[32,256]{1,0:T(8,128)}) %reduce-scatter.33.cloned.1.call-update) | async-done | bytes 32784 | tf_op jit(solution)/shard_map/reduce_scatter | solution.py:21
  371.1 13.1 %all_gather.47 = bf16[32,1024]{1,0:T(8,128)(2,1)S(1)} all-gather(bf16[32,256]{1,0:T(8,128)(2,1)S(1)} %subtract_convert_fusion), channel_id=1, replica_groups=mesh['freq'=2,'base'=4,'pix'=4] {'pix'}, dimensions={1}, use_global_device_ids=true | all-gather | bytes 81920 | tf_op jit(solution)/shard_map/all_gather | solution.py:26
  385.7 17.4 %reduce-scatter.35.cloned.1.call-done = f32[32,128]{1,0:T(8,128)} async-done(((f32[32,512]{1,0:T(8,128)}), f32[32,128]{1,0:T(8,128)}) %reduce-scatter.35.cloned.1.call-update) | async-done | bytes 16400 | tf_op jit(solution)/shard_map/reduce_scatter | solution.py:45
  (80 shorter events, 62.2 us)
Async XLA Ops:
  6.5 7.0 %copy-start = (bf16[1,1024,512]{2,1,0:T(8,128)(2,1)S(1)}, bf16[1,1024,512]{2,1,0:T(8,128)(2,1)}, u32[]{:S(2)}) copy-start(bf16[1,1024,512]{2,1,0:T(8,128)(2,1)} %param.4) | copy-start | bytes 3145732
  6.5 29.4 %reduce-scatter.13.cloned.1.call-start = ((), (), s32[]{:S(2)}) async-start(), calls=%async_computation.12 | async-start | bytes 163840 | tf_op jit(solution)/shard_map/reduce_scatter | solution.py:21
  14.5 21.4 %copy-start.1 = (f32[32,1024]{1,0:T(8,128)S(1)}, f32[32,1024]{1,0:T(8,128)}, u32[]{:S(2)}) copy-start(f32[32,1024]{1,0:T(8,128)} %param.5) | copy-start | bytes 393220
  14.6 54.1 %reduce-scatter.15.cloned.1.call-start = ((), (), s32[]{:S(2)}) async-start(), calls=%async_computation.13 | async-start | bytes 81920 | tf_op jit(solution)/shard_map/reduce_scatter | solution.py:45
  50.7 0.7 copy-start.4
  50.7 17.9 %copy-start.2 = (f32[32,1,1,128]{3,2,1,0:T(1,128)S(1)}, f32[32,1,1,128]{3,2,1,0:T(1,128)}, u32[]{:S(2)}) copy-start(f32[32,1,1,128]{3,2,1,0:T(1,128)} %param.6) | copy-start | bytes 49156
  50.8 52.0 %reduce-scatter.17.cloned.1.call-start = ((), (), s32[]{:S(2)}) async-start(), calls=%async_computation.14 | async-start | bytes 163840 | tf_op jit(solution)/shard_map/reduce_scatter | solution.py:21
  70.0 6.8 %copy-start.3 = (f32[32,128]{1,0:T(8,128)S(1)}, f32[32,128]{1,0:T(8,128)}, u32[]{:S(2)}) copy-start(f32[32,128]{1,0:T(8,128)} %reduce-scatter.15.cloned.1.call-done) | copy-start | bytes 49156
  83.2 52.3 %reduce-scatter.19.cloned.1.call-start = ((), (), s32[]{:S(2)}) async-start(), calls=%async_computation.15 | async-start | bytes 81920 | tf_op jit(solution)/shard_map/reduce_scatter | solution.py:45
  117.6 52.1 %reduce-scatter.21.cloned.1.call-start = ((), (), s32[]{:S(2)}) async-start(), calls=%async_computation.16 | async-start | bytes 163840 | tf_op jit(solution)/shard_map/reduce_scatter | solution.py:21
  150.1 52.3 %reduce-scatter.23.cloned.1.call-start = ((), (), s32[]{:S(2)}) async-start(), calls=%async_computation.17 | async-start | bytes 81920 | tf_op jit(solution)/shard_map/reduce_scatter | solution.py:45
  184.5 52.1 %reduce-scatter.25.cloned.1.call-start = ((), (), s32[]{:S(2)}) async-start(), calls=%async_computation.18 | async-start | bytes 163840 | tf_op jit(solution)/shard_map/reduce_scatter | solution.py:21
  217.0 52.3 %reduce-scatter.27.cloned.1.call-start = ((), (), s32[]{:S(2)}) async-start(), calls=%async_computation.19 | async-start | bytes 81920 | tf_op jit(solution)/shard_map/reduce_scatter | solution.py:45
  251.4 52.1 %reduce-scatter.29.cloned.1.call-start = ((), (), s32[]{:S(2)}) async-start(), calls=%async_computation.20 | async-start | bytes 163840 | tf_op jit(solution)/shard_map/reduce_scatter | solution.py:21
  283.9 52.3 %reduce-scatter.31.cloned.1.call-start = ((), (), s32[]{:S(2)}) async-start(), calls=%async_computation.21 | async-start | bytes 81920 | tf_op jit(solution)/shard_map/reduce_scatter | solution.py:45
  318.3 52.1 %reduce-scatter.33.cloned.1.call-start = ((), (), s32[]{:S(2)}) async-start(), calls=%async_computation.22 | async-start | bytes 163840 | tf_op jit(solution)/shard_map/reduce_scatter | solution.py:21
  350.7 52.3 %reduce-scatter.35.cloned.1.call-start = ((), (), s32[]{:S(2)}) async-start(), calls=%async_computation.23 | async-start | bytes 81920 | tf_op jit(solution)/shard_map/reduce_scatter | solution.py:45
  404.5 6.8 %copy-start.5 = (f32[32,128]{1,0:T(8,128)S(1)}, f32[32,128]{1,0:T(8,128)}, u32[]{:S(2)}) copy-start(f32[32,128]{1,0:T(8,128)} %reduce-scatter.35.cloned.1.call-done) | copy-start | bytes 49156
Sparse Core Ops, SparseCore 0:
  14.7 21.1 reduce-scatter.12
  50.9 17.7 reduce-scatter.14
  83.3 19.4 reduce-scatter.16
  117.7 17.7 reduce-scatter.18
  150.2 19.4 reduce-scatter.20
  184.6 17.7 reduce-scatter.22
  217.1 19.4 reduce-scatter.24
  251.5 17.7 reduce-scatter.26
  284.0 19.4 reduce-scatter.28
  318.4 17.7 reduce-scatter.30
  350.9 19.4 reduce-scatter.32
  385.3 17.7 reduce-scatter.34
where the time goes:
time: 420 us; the launch traced here: 419 us
  waiting for transfers between devices  223 us (53%)
  blocking collectives  144 us (34%)
  between operations  21.7 us (5%)
  other arithmetic  17.7 us (4%)
  matrix products  11.8 us (3%)
    reduce_scatter x6, waiting for transfers between devices, residual_of(): lax.psum_scatter(partial_value, 'pix', scatter_dimension=1, tiled=True)  119 us
    reduce_scatter x6, waiting for transfers between devices, on_device(): lax.psum_scatter(gradient_portion, 'base', scatter_dimension=1, tiled=True)  103 us
    all_gather x6, blocking collectives, residual_of(): lax.all_gather((own_rows - shares).astype(jnp.bfloat16), 'pix', axis=1, t...  78.7 us
    psum x6, blocking collectives, on_device(): total = lax.psum(local_sum, 'freq')  33.2 us
    all_gather x6, blocking collectives, on_device(): lax.all_gather(rounded_amount, 'base', axis=1, tiled=True)  32 us
    reduce_sum x6, other arithmetic, on_device(): local_sum = jnp.sum(tiles * tiles, axis=(0, 2))  8.45 us
  transfers between devices with their start and end apart: 12, of which 12 were waited for; matrix products, arithmetic and copies ran while one was open for 1% of the time, Pallas kernels for 0%

commit v1 on v0

--- a/solution.py
+++ b/solution.py
@@ -46,7 +46,7 @@
         moved = current + descent_stride * grad_share
         tiles = moved.reshape(chans, tiles_share, TILE)
         local_sum = jnp.sum(tiles * tiles, axis=(0, 2))
-        total = lax.psum(local_sum, "freq")
+        total = lax.all_gather(local_sum, "freq").sum(axis=0)
         ranks = lax.dynamic_slice_in_dim(
             patch_order_record[step], base_index * tiles_share, tiles_share, 0
         )

time: 420 us -> 429 us (1.021)
  local copies, waits for them, and re-layouts: 0.69 us -> 10.5 us
    psum x6 -> x0, blocking collectives: 33.2 us -> none  [on_device(): total = lax.psum(local_sum, 'freq')]
    unnamed x0 -> x6, blocking collectives: none -> 29.5 us
    unnamed x12 -> x27, local copies, waits for them, and re-layouts: 0.62 us -> 10.5 us
where the time goes in v1:
time: 429 us; the launch traced here: 428 us
  waiting for transfers between devices  223 us (52%)
  blocking collectives  140 us (33%)
  between operations  21.9 us (5%)
  other arithmetic  20.1 us (5%)
  matrix products  11.8 us (3%)
  local copies, waits for them, and re-layouts  10.5 us (2%)
    reduce_scatter x6, waiting for transfers between devices, residual_of(): lax.psum_scatter(partial_value, 'pix', scatter_dimension=1, tiled=True)  118 us
    reduce_scatter x6, waiting for transfers between devices, on_device(): lax.psum_scatter(gradient_portion, 'base', scatter_dimension=1, tiled=True)  105 us
    all_gather x6, blocking collectives, residual_of(): lax.all_gather((own_rows - shares).astype(jnp.bfloat16), 'pix', axis=1, t...  78.7 us
    all_gather x6, blocking collectives, on_device(): lax.all_gather(rounded_amount, 'base', axis=1, tiled=True)  32 us
    unnamed x6, blocking collectives  29.5 us
    unnamed x27, local copies, waits for them, and re-layouts  10.5 us
  transfers between devices with their start and end apart: 12, of which 12 were waited for; matrix products, arithmetic and copies ran while one was open for 1% of the time, Pallas kernels for 0%

profile of v1, /device:TPU:0, one launch (start us, length us, event | category | flops | bytes accessed | tf_op | source)
XLA Modules:
  0.0 427.7 jit_solution(5896169883992012230)
XLA Ops:
  7.3 6.1 %all_gather.72 = bf16[32,512]{1,0:T(8,128)(2,1)S(1)} all-gather(bf16[32,128]{1,0:T(8,128)(2,1)S(1)} %convert_element_type.42), channel_id=1, replica_groups=mesh['freq'=2,'base'=4,'pix'=4] {'base'}, dimensions={1}, use_global_device_ids=true | all-gather | bytes 40960 | tf_op jit(solution)/shard_map/all_gather | solution.py:41
  15.9 20.0 %reduce-scatter.13.cloned.1.call-done = f32[32,256]{1,0:T(8,128)} async-done(((f32[32,1024]{1,0:T(8,128)}), f32[32,256]{1,0:T(8,128)}) %reduce-scatter.13.cloned.1.call-update) | async-done | bytes 32784 | tf_op jit(solution)/shard_map/reduce_scatter | solution.py:21
  36.7 13.1 %all_gather.73 = bf16[32,1024]{1,0:T(8,128)(2,1)S(1)} all-gather(bf16[32,256]{1,0:T(8,128)(2,1)S(1)} %subtract_convert_fusion.5), channel_id=1, replica_groups=mesh['freq'=2,'base'=4,'pix'=4] {'pix'}, dimensions={1}, use_global_device_ids=true | all-gather | bytes 81920 | tf_op jit(solution)/shard_map/all_gather | solution.py:26
  52.0 16.6 %reduce-scatter.15.cloned.1.call-done = f32[32,128]{1,0:T(8,128)} async-done(((f32[32,512]{1,0:T(8,128)}), f32[32,128]{1,0:T(8,128)}) %reduce-scatter.15.cloned.1.call-update) | async-done | bytes 16400 | tf_op jit(solution)/shard_map/reduce_scatter | solution.py:45
  78.5 5.2 %all_gather.76 = bf16[32,512]{1,0:T(8,128)(2,1)S(1)} all-gather(bf16[32,128]{1,0:T(8,128)(2,1)S(1)} %multiply_convert_fusion.4), channel_id=1, replica_groups=mesh['freq'=2,'base'=4,'pix'=4] {'base'}, dimensions={1}, use_global_device_ids=true | all-gather | bytes 40960 | tf_op jit(solution)/shard_map/all_gather | solution.py:41
  84.8 19.6 %reduce-scatter.17.cloned.1.call-done = f32[32,256]{1,0:T(8,128)} async-done(((f32[32,1024]{1,0:T(8,128)}), f32[32,256]{1,0:T(8,128)}) %reduce-scatter.17.cloned.1.call-update) | async-done | bytes 32784 | tf_op jit(solution)/shard_map/reduce_scatter | solution.py:21
  105.2 13.1 %all_gather.77 = bf16[32,1024]{1,0:T(8,128)(2,1)S(1)} all-gather(bf16[32,256]{1,0:T(8,128)(2,1)S(1)} %subtract_convert_fusion.4), channel_id=1, replica_groups=mesh['freq'=2,'base'=4,'pix'=4] {'pix'}, dimensions={1}, use_global_device_ids=true | all-gather | bytes 81920 | tf_op jit(solution)/shard_map/all_gather | solution.py:26
  119.8 17.3 %reduce-scatter.19.cloned.1.call-done = f32[32,128]{1,0:T(8,128)} async-done(((f32[32,512]{1,0:T(8,128)}), f32[32,128]{1,0:T(8,128)}) %reduce-scatter.19.cloned.1.call-update) | async-done | bytes 16400 | tf_op jit(solution)/shard_map/reduce_scatter | solution.py:45
  146.7 5.2 %all_gather.80 = bf16[32,512]{1,0:T(8,128)(2,1)S(1)} all-gather(bf16[32,128]{1,0:T(8,128)(2,1)S(1)} %multiply_convert_fusion.3), channel_id=1, replica_groups=mesh['freq'=2,'base'=4,'pix'=4] {'base'}, dimensions={1}, use_global_device_ids=true | all-gather | bytes 40960 | tf_op jit(solution)/shard_map/all_gather | solution.py:41
  153.0 19.6 %reduce-scatter.21.cloned.1.call-done = f32[32,256]{1,0:T(8,128)} async-done(((f32[32,1024]{1,0:T(8,128)}), f32[32,256]{1,0:T(8,128)}) %reduce-scatter.21.cloned.1.call-update) | async-done | bytes 32784 | tf_op jit(solution)/shard_map/reduce_scatter | solution.py:21
  173.4 13.1 %all_gather.81 = bf16[32,1024]{1,0:T(8,128)(2,1)S(1)} all-gather(bf16[32,256]{1,0:T(8,128)(2,1)S(1)} %subtract_convert_fusion.3), channel_id=1, replica_groups=mesh['freq'=2,'base'=4,'pix'=4] {'pix'}, dimensions={1}, use_global_device_ids=true | all-gather | bytes 81920 | tf_op jit(solution)/shard_map/all_gather | solution.py:26
  187.5 17.8 %reduce-scatter.23.cloned.1.call-done = f32[32,128]{1,0:T(8,128)} async-done(((f32[32,512]{1,0:T(8,128)}), f32[32,128]{1,0:T(8,128)}) %reduce-scatter.23.cloned.1.call-update) | async-done | bytes 16400 | tf_op jit(solution)/shard_map/reduce_scatter | solution.py:45
  215.2 5.2 %all_gather.84 = bf16[32,512]{1,0:T(8,128)(2,1)S(1)} all-gather(bf16[32,128]{1,0:T(8,128)(2,1)S(1)} %multiply_convert_fusion.2), channel_id=1, replica_groups=mesh['freq'=2,'base'=4,'pix'=4] {'base'}, dimensions={1}, use_global_device_ids=true | all-gather | bytes 40960 | tf_op jit(solution)/shard_map/all_gather | solution.py:41
  221.5 19.6 %reduce-scatter.25.cloned.1.call-done = f32[32,256]{1,0:T(8,128)} async-done(((f32[32,1024]{1,0:T(8,128)}), f32[32,256]{1,0:T(8,128)}) %reduce-scatter.25.cloned.1.call-update) | async-done | bytes 32784 | tf_op jit(solution)/shard_map/reduce_scatter | solution.py:21
  241.8 13.1 %all_gather.85 = bf16[32,1024]{1,0:T(8,128)(2,1)S(1)} all-gather(bf16[32,256]{1,0:T(8,128)(2,1)S(1)} %subtract_convert_fusion.2), channel_id=1, replica_groups=mesh['freq'=2,'base'=4,'pix'=4] {'pix'}, dimensions={1}, use_global_device_ids=true | all-gather | bytes 81920 | tf_op jit(solution)/shard_map/all_gather | solution.py:26
  256.4 17.3 %reduce-scatter.27.cloned.1.call-done = f32[32,128]{1,0:T(8,128)} async-done(((f32[32,512]{1,0:T(8,128)}), f32[32,128]{1,0:T(8,128)}) %reduce-scatter.27.cloned.1.call-update) | async-done | bytes 16400 | tf_op jit(solution)/shard_map/reduce_scatter | solution.py:45
  283.3 5.2 %all_gather.88 = bf16[32,512]{1,0:T(8,128)(2,1)S(1)} all-gather(bf16[32,128]{1,0:T(8,128)(2,1)S(1)} %multiply_convert_fusion.1), channel_id=1, replica_groups=mesh['freq'=2,'base'=4,'pix'=4] {'base'}, dimensions={1}, use_global_device_ids=true | all-gather | bytes 40960 | tf_op jit(solution)/shard_map/all_gather | solution.py:41
  289.7 19.6 %reduce-scatter.29.cloned.1.call-done = f32[32,256]{1,0:T(8,128)} async-done(((f32[32,1024]{1,0:T(8,128)}), f32[32,256]{1,0:T(8,128)}) %reduce-scatter.29.cloned.1.call-update) | async-done | bytes 32784 | tf_op jit(solution)/shard_map/reduce_scatter | solution.py:21
  310.0 13.1 %all_gather.89 = bf16[32,1024]{1,0:T(8,128)(2,1)S(1)} all-gather(bf16[32,256]{1,0:T(8,128)(2,1)S(1)} %subtract_convert_fusion.1), channel_id=1, replica_groups=mesh['freq'=2,'base'=4,'pix'=4] {'pix'}, dimensions={1}, use_global_device_ids=true | all-gather | bytes 81920 | tf_op jit(solution)/shard_map/all_gather | solution.py:26
  324.1 17.8 %reduce-scatter.31.cloned.1.call-done = f32[32,128]{1,0:T(8,128)} async-done(((f32[32,512]{1,0:T(8,128)}), f32[32,128]{1,0:T(8,128)}) %reduce-scatter.31.cloned.1.call-update) | async-done | bytes 16400 | tf_op jit(solution)/shard_map/reduce_scatter | solution.py:45
  351.8 5.2 %all_gather.92 = bf16[32,512]{1,0:T(8,128)(2,1)S(1)} all-gather(bf16[32,128]{1,0:T(8,128)(2,1)S(1)} %multiply_convert_fusion), channel_id=1, replica_groups=mesh['freq'=2,'base'=4,'pix'=4] {'base'}, dimensions={1}, use_global_device_ids=true | all-gather | bytes 40960 | tf_op jit(solution)/shard_map/all_gather | solution.py:41
  358.1 19.5 %reduce-scatter.33.cloned.1.call-done = f32[32,256]{1,0:T(8,128)} async-done(((f32[32,1024]{1,0:T(8,128)}), f32[32,256]{1,0:T(8,128)}) %reduce-scatter.33.cloned.1.call-update) | async-done | bytes 32784 | tf_op jit(solution)/shard_map/reduce_scatter | solution.py:21
  378.4 13.1 %all_gather.93 = bf16[32,1024]{1,0:T(8,128)(2,1)S(1)} all-gather(bf16[32,256]{1,0:T(8,128)(2,1)S(1)} %subtract_convert_fusion), channel_id=1, replica_groups=mesh['freq'=2,'base'=4,'pix'=4] {'pix'}, dimensions={1}, use_global_device_ids=true | all-gather | bytes 81920 | tf_op jit(solution)/shard_map/all_gather | solution.py:26
  392.4 17.9 %reduce-scatter.35.cloned.1.call-done = f32[32,128]{1,0:T(8,128)} async-done(((f32[32,512]{1,0:T(8,128)}), f32[32,128]{1,0:T(8,128)}) %reduce-scatter.35.cloned.1.call-update) | async-done | bytes 16400 | tf_op jit(solution)/shard_map/reduce_scatter | solution.py:45
  (98 shorter events, 72.5 us)
Async XLA Ops:
  6.5 7.0 %copy-start = (bf16[1,1024,512]{2,1,0:T(8,128)(2,1)S(1)}, bf16[1,1024,512]{2,1,0:T(8,128)(2,1)}, u32[]{:S(2)}) copy-start(bf16[1,1024,512]{2,1,0:T(8,128)(2,1)} %param.4) | copy-start | bytes 3145732
  6.5 29.4 %reduce-scatter.13.cloned.1.call-start = ((), (), s32[]{:S(2)}) async-start(), calls=%async_computation.12 | async-start | bytes 163840 | tf_op jit(solution)/shard_map/reduce_scatter | solution.py:21
  14.5 21.4 %copy-start.1 = (f32[32,1024]{1,0:T(8,128)S(1)}, f32[32,1024]{1,0:T(8,128)}, u32[]{:S(2)}) copy-start(f32[32,1024]{1,0:T(8,128)} %param.5) | copy-start | bytes 393220
  14.6 54.1 %reduce-scatter.15.cloned.1.call-start = ((), (), s32[]{:S(2)}) async-start(), calls=%async_computation.13 | async-start | bytes 81920 | tf_op jit(solution)/shard_map/reduce_scatter | solution.py:45
  14.6 0.7 copy-start.6
  50.7 0.7 copy-start.4
  50.8 17.9 %copy-start.2 = (f32[32,1,1,128]{3,2,1,0:T(1,128)S(1)}, f32[32,1,1,128]{3,2,1,0:T(1,128)}, u32[]{:S(2)}) copy-start(f32[32,1,1,128]{3,2,1,0:T(1,128)} %param.6) | copy-start | bytes 49156
  50.8 53.6 %reduce-scatter.17.cloned.1.call-start = ((), (), s32[]{:S(2)}) async-start(), calls=%async_computation.14 | async-start | bytes 163840 | tf_op jit(solution)/shard_map/reduce_scatter | solution.py:21
  70.1 8.4 %copy-start.3 = (f32[32,128]{1,0:T(8,128)S(1)}, f32[32,128]{1,0:T(8,128)}, u32[]{:S(2)}) copy-start(f32[32,128]{1,0:T(8,128)} %reduce-scatter.15.cloned.1.call-done) | copy-start | bytes 49156
  84.8 52.3 %reduce-scatter.19.cloned.1.call-start = ((), (), s32[]{:S(2)}) async-start(), calls=%async_computation.15 | async-start | bytes 81920 | tf_op jit(solution)/shard_map/reduce_scatter | solution.py:45
  119.2 53.4 %reduce-scatter.21.cloned.1.call-start = ((), (), s32[]{:S(2)}) async-start(), calls=%async_computation.16 | async-start | bytes 163840 | tf_op jit(solution)/shard_map/reduce_scatter | solution.py:21
  153.0 52.3 %reduce-scatter.23.cloned.1.call-start = ((), (), s32[]{:S(2)}) async-start(), calls=%async_computation.17 | async-start | bytes 81920 | tf_op jit(solution)/shard_map/reduce_scatter | solution.py:45
  187.4 53.6 %reduce-scatter.25.cloned.1.call-start = ((), (), s32[]{:S(2)}) async-start(), calls=%async_computation.18 | async-start | bytes 163840 | tf_op jit(solution)/shard_map/reduce_scatter | solution.py:21
  221.4 52.3 %reduce-scatter.27.cloned.1.call-start = ((), (), s32[]{:S(2)}) async-start(), calls=%async_computation.19 | async-start | bytes 81920 | tf_op jit(solution)/shard_map/reduce_scatter | solution.py:45
  255.8 53.4 %reduce-scatter.29.cloned.1.call-start = ((), (), s32[]{:S(2)}) async-start(), calls=%async_computation.20 | async-start | bytes 163840 | tf_op jit(solution)/shard_map/reduce_scatter | solution.py:21
  289.6 52.3 %reduce-scatter.31.cloned.1.call-start = ((), (), s32[]{:S(2)}) async-start(), calls=%async_computation.21 | async-start | bytes 81920 | tf_op jit(solution)/shard_map/reduce_scatter | solution.py:45
  324.0 53.6 %reduce-scatter.33.cloned.1.call-start = ((), (), s32[]{:S(2)}) async-start(), calls=%async_computation.22 | async-start | bytes 163840 | tf_op jit(solution)/shard_map/reduce_scatter | solution.py:21
  358.0 52.3 %reduce-scatter.35.cloned.1.call-start = ((), (), s32[]{:S(2)}) async-start(), calls=%async_computation.23 | async-start | bytes 81920 | tf_op jit(solution)/shard_map/reduce_scatter | solution.py:45
  411.8 8.5 %copy-start.5 = (f32[32,128]{1,0:T(8,128)S(1)}, f32[32,128]{1,0:T(8,128)}, u32[]{:S(2)}) copy-start(f32[32,128]{1,0:T(8,128)} %reduce-scatter.35.cloned.1.call-done) | copy-start | bytes 49156
Sparse Core Ops, SparseCore 0:
  14.7 21.1 reduce-scatter.12
  50.9 17.7 reduce-scatter.14
  84.9 19.4 reduce-scatter.16
  119.3 17.7 reduce-scatter.18
  153.1 19.4 reduce-scatter.20
  187.5 17.7 reduce-scatter.22
  221.5 19.4 reduce-scatter.24
  256.0 17.7 reduce-scatter.26
  289.7 19.4 reduce-scatter.28
  324.1 17.7 reduce-scatter.30
  358.1 19.4 reduce-scatter.32
  392.5 17.7 reduce-scatter.34
